TPU v7x, 32 devices: a whole 2x2x4 slice. The times are simulated.
32 devices in a mesh: seq: 8 (over z, core), fsdp: 4 (over y, x).
Axes of the slice: x: 2, y: 2, z: 4, core: 2. Of those that a mesh axis runs over, the one named last changes fastest.
Arguments:
- tokens: bfloat16 [4, 2048, 1536], P('fsdp', 'seq'), may hold values from -6 to 6
- seg_ids: int32 [4, 2048], P('fsdp'), may hold values from 0 to 3, never falling along the last dimension, each value on 1 to 1024 neighbouring positions
- pre_gain: float32 [1536], replicated, may hold values from 0.25 to 1.75
- w_in: bfloat16 [1536, 6448], P('fsdp'), may hold values from -0.15625 to 0.15625
- conv_weight: float32 [4, 3328], replicated, may hold values from -3 to 3
- conv_bias: float32 [3328], replicated, may hold values from -3 to 3
- dt_bias: float32 [48], replicated, may hold values from -6 to -2
- a_log: float32 [48], replicated, may hold values from -5 to 1.5
- d_skip: float32 [48], replicated, may hold values from 0 to 2
- norm_gain: float32 [3072], replicated, may hold values from 0.25 to 1.75
- w_out: bfloat16 [3072, 1536], P('fsdp'), may hold values from -0.109375 to 0.109375
- cotangent: bfloat16 [4, 2048, 1536], P('fsdp', 'seq'), may hold values from -6 to 6
Outputs:
- output: bfloat16 [4, 2048, 1536], P('fsdp', 'seq')
- input_grad: bfloat16 [4, 2048, 1536], P('fsdp', 'seq')
- grad_in_w: float32 [1536, 6448], P('fsdp')
- grad_out_w: float32 [3072, 1536], P('fsdp')
- grad_pre_gain: float32 [1536], replicated
- grad_conv_weight: float32 [4, 3328], replicated
- grad_conv_bias: float32 [3328], replicated
- grad_dt_bias: float32 [48], replicated
- grad_a_log: float32 [48], replicated
- grad_d_skip: float32 [48], replicated
- grad_norm_gain: float32 [3072], replicated
Inputs may be any that keep to these rules, and one draw needn't show every extreme that they name: `seg_ids`: along each sequence the document numbers never fall; each document holds at most 1024 positions and one holds exactly that many.
All inputs are finite; a program needn't handle non-finite values.
Results may differ from a plain program's by a relative error of at most 0.012.
The roundings to bfloat16 on the way count: a program that leaves them out, or rounds other values in their place, can miss the bound.
Values may be sent and summed in bfloat16 or wider, within the bound.
A program may use at most 256 MiB of HBM per device.

v0:
```python
import jax
import jax.numpy as jnp
from jax import lax
from jax.sharding import PartitionSpec as P

P_SIZE = 64
N = 128
SPAN = 256


EPSILON = 1e-05
HIGHEST = lax.Precision.HIGHEST


def causal_conv(values, kernel, offset_bias, segment):
    length = values.shape[0]
    taps = kernel.shape[0]
    padded = jnp.pad(values, ((taps - 1, 0), (0, 0)))
    seg_padded = jnp.pad(segment, (taps - 1, 0), constant_values=-1)
    total = jnp.zeros_like(values) + offset_bias[None, :]
    for lag_index in range(taps):
        same_doc = (seg_padded[lag_index : lag_index + length] == segment).astype(jnp.float32)
        total = (
            total
            + kernel[lag_index][None, :]
            * padded[lag_index : lag_index + length]
            * same_doc[:, None]
        )
    return jax.nn.silu(total)


def mixer(
    x_raw,
    bc_raw,
    dt_raw,
    kernel_x,
    bias_x,
    kernel_bc,
    bias_bc,
    step_bias,
    decay_log,
    skip_weight,
    segment,
):
    length = x_raw.shape[0]
    head_count = dt_raw.shape[1]
    x_conv = causal_conv(x_raw, kernel_x, bias_x, segment)
    bc_conv = causal_conv(bc_raw, kernel_bc, bias_bc, segment)
    key_rows = bc_conv[:, :N]
    query_rows = bc_conv[:, N:]
    step_size = jax.nn.softplus(dt_raw + step_bias[None, :])
    rate = -step_size * jnp.exp(decay_log)[None, :]
    blocks = length // SPAN
    x_blocks = x_conv.reshape(blocks, SPAN, head_count, P_SIZE)
    key_blocks = key_rows.reshape(blocks, SPAN, N)
    query_blocks = query_rows.reshape(blocks, SPAN, N)
    step_blocks = step_size.reshape(blocks, SPAN, head_count)
    rate_blocks = rate.reshape(blocks, SPAN, head_count)
    seg_blocks = segment.reshape(blocks, SPAN)
    cumulative = jnp.cumsum(rate_blocks, axis=1)
    scores = jnp.einsum("cqn,ckn->cqk", query_blocks, key_blocks, precision=HIGHEST)
    causal = jnp.arange(SPAN)[:, None] >= jnp.arange(SPAN)[None, :]
    live = causal[None] & (seg_blocks[:, :, None] == seg_blocks[:, None, :])
    gap = cumulative[:, :, None, :] - cumulative[:, None, :, :]
    decay = jnp.exp(jnp.where(live[..., None], gap, -1000000000.0))
    mixing = scores[..., None] * decay * step_blocks[:, None, :, :]
    inside = jnp.einsum("cqkh,ckhp->cqhp", mixing, x_blocks, precision=HIGHEST)
    last_seg = seg_blocks[:, -1]
    to_end = (
        jnp.exp(cumulative[:, -1:, :] - cumulative)
        * (seg_blocks == last_seg[:, None]).astype(jnp.float32)[..., None]
    )
    states = jnp.einsum(
        "ckn,ckh,ckhp->chnp", key_blocks, to_end * step_blocks, x_blocks, precision=HIGHEST
    )
    through = jnp.exp(cumulative[:, -1, :])
    keeping = jnp.concatenate(
        [jnp.zeros((1,), jnp.float32), (last_seg[1:] == last_seg[:-1]).astype(jnp.float32)]
    )

    def carry_step(previous, pieces):
        state_now, passed, kept = pieces
        updated = state_now + previous * (passed * kept)[:, None, None]
        return (updated, previous)

    _, entering = lax.scan(
        carry_step, jnp.zeros((head_count, N, P_SIZE), jnp.float32), (states, through, keeping)
    )
    prev_seg = jnp.concatenate([last_seg[:1] * 0 - 1, last_seg[:-1]])
    from_prev = (
        jnp.exp(cumulative) * (seg_blocks == prev_seg[:, None]).astype(jnp.float32)[..., None]
    )
    carried = (
        jnp.einsum("cqn,chnp->cqhp", query_blocks, entering, precision=HIGHEST)
        * from_prev[..., None]
    )
    result = inside + carried + skip_weight[None, None, :, None] * x_blocks
    return result.reshape(length, head_count * P_SIZE)


def shards(
    tokens,
    seg_ids,
    pre_gain,
    w_in,
    conv_weight,
    conv_bias,
    dt_bias,
    a_log,
    d_skip,
    norm_gain,
    w_out,
    cotangent,
):
    seq_count = lax.axis_size("seq")
    seq_index = lax.axis_index("seq")
    local_len = tokens.shape[1]
    inner = norm_gain.shape[0]
    head_total = dt_bias.shape[0]
    state_pair = conv_bias.shape[0] - inner
    taps = conv_weight.shape[0]
    head_local = head_total // seq_count
    chan_local = inner // seq_count
    chan_start = seq_index * chan_local
    head_start = seq_index * head_local
    segment = seg_ids[0]
    full_in, full_out = (
        lax.all_gather(w_in, "fsdp", axis=0, tiled=True),
        lax.all_gather(w_out, "fsdp", axis=0, tiled=True),
    )
    tok_float = tokens[0].astype(jnp.float32)
    inv_rms = lax.rsqrt(jnp.mean(tok_float * tok_float, -1, keepdims=True) + EPSILON)
    scaled = tok_float * inv_rms
    normed = (scaled * pre_gain[None, :]).astype(jnp.bfloat16)
    projected = jnp.dot(normed, full_in, preferred_element_type=jnp.float32).astype(jnp.bfloat16)
    moved = projected[:, : 2 * inner].reshape(1, local_len, 2, inner)
    dt_moved = projected[:, 2 * inner + state_pair :].reshape(1, local_len, 1, head_total)
    head_side, dt_heads = (
        lax.all_to_all(moved, "seq", split_axis=3, concat_axis=1, tiled=True),
        lax.all_to_all(dt_moved, "seq", split_axis=3, concat_axis=1, tiled=True),
    )
    bc_local = projected[:, 2 * inner : 2 * inner + state_pair].reshape(1, local_len, state_pair)
    bc_full = lax.all_gather(bc_local, "seq", axis=1, tiled=True)
    kernel_x = lax.dynamic_slice_in_dim(conv_weight[:, :inner], chan_start, chan_local, 1)
    bias_x = lax.dynamic_slice_in_dim(conv_bias[:inner], chan_start, chan_local, 0)
    mixer_args = (
        head_side[0, :, -1].astype(jnp.float32),
        bc_full[0].astype(jnp.float32),
        dt_heads[0, :, 0].astype(jnp.float32),
        kernel_x,
        bias_x,
        conv_weight[:, inner:],
        conv_bias[inner:],
        lax.dynamic_slice_in_dim(dt_bias, head_start, head_local, 0),
        lax.dynamic_slice_in_dim(a_log, head_start, head_local, 0),
        lax.dynamic_slice_in_dim(d_skip, head_start, head_local, 0),
    )
    mixed, pullback = jax.vjp(lambda *values: mixer(*values, segment), *mixer_args)
    mixed_half = mixed.astype(jnp.bfloat16)
    y_float = lax.optimization_barrier(mixed_half).astype(jnp.float32)
    z_float = head_side[0, :, 0].astype(jnp.float32)
    gain_part = lax.dynamic_slice_in_dim(norm_gain, chan_start, chan_local, 0)
    sigma = jax.nn.sigmoid(z_float)
    gated_z = z_float * sigma
    gated = y_float * gated_z
    square_sum = lax.psum(jnp.sum(gated * gated, -1), "seq")
    inv_gate = lax.rsqrt(square_sum[:, None] / inner + EPSILON)
    unit_gate = gated * inv_gate
    sent = (unit_gate * gain_part[None, :]).astype(jnp.bfloat16)[None]
    returned = lax.all_to_all(sent, "seq", split_axis=1, concat_axis=2, tiled=True)[0]
    output = (tok_float + jnp.dot(returned, full_out, preferred_element_type=jnp.float32)).astype(
        jnp.bfloat16
    )
    cot_half = cotangent[0]
    cot_float = cot_half.astype(jnp.float32)
    grad_gate_half = jnp.dot(cot_half, full_out.T, preferred_element_type=jnp.float32).astype(
        jnp.bfloat16
    )
    grad_sent = grad_gate_half[None]
    grad_arrived = lax.all_to_all(grad_sent, "seq", split_axis=2, concat_axis=1, tiled=True)[0]
    grad_gate = grad_arrived.astype(jnp.float32)
    ngain_local = jnp.sum(grad_gate * unit_gate, 0)
    scaled_grad = grad_gate * gain_part[None, :]
    inner_sum = lax.psum(jnp.sum(scaled_grad * unit_gate, -1), "seq")
    grad_gated = inv_gate * (scaled_grad - unit_gate * (inner_sum[:, None] / inner))
    grad_y_half = (grad_gated * gated_z).astype(jnp.bfloat16)
    grad_z_half = (grad_gated * y_float * sigma * (1.0 + z_float * (1.0 - sigma))).astype(
        jnp.bfloat16
    )
    grad_ngain = lax.dynamic_update_slice_in_dim(
        jnp.zeros((inner,), jnp.float32), ngain_local, chan_start, 0
    )
    grad_y = lax.optimization_barrier(grad_y_half).astype(jnp.float32)
    g_x, g_bc, g_dt, g_kx, g_bx, g_kbc, g_bbc, g_step, g_decay, g_skip = pullback(grad_y)
    x_grad_half = g_x.astype(jnp.bfloat16)
    dt_grad_half = g_dt.astype(jnp.bfloat16)[None, :, None, :]
    back_moved = jnp.stack([grad_z_half, x_grad_half], 1)[None]
    zx_grad, dt_grad = (
        lax.all_to_all(back_moved, "seq", split_axis=1, concat_axis=3, tiled=True),
        lax.all_to_all(dt_grad_half, "seq", split_axis=1, concat_axis=3, tiled=True),
    )
    bc_grad = lax.psum_scatter(g_bc[None], "seq", scatter_dimension=1, tiled=True)[0].astype(
        jnp.bfloat16
    )
    zx_flat = zx_grad[0].reshape(local_len, 2 * inner)
    proj_grad = jnp.concatenate([zx_flat, bc_grad, dt_grad[0, :, 0]], -1)
    grad_normed = jnp.dot(proj_grad, full_in.T, preferred_element_type=jnp.float32)
    grad_pre = jnp.sum(grad_normed * scaled, 0)
    weighted = grad_normed * pre_gain[None, :]
    input_grad = (
        cot_float + inv_rms * (weighted - scaled * jnp.mean(weighted * scaled, -1, keepdims=True))
    ).astype(jnp.bfloat16)
    conv_x_grad = lax.dynamic_update_slice_in_dim(
        jnp.zeros((taps, inner), jnp.float32), g_kx, chan_start, 1
    )
    conv_w_grad = jnp.concatenate([conv_x_grad, g_kbc], 1)
    bias_x_grad = lax.dynamic_update_slice_in_dim(
        jnp.zeros((inner,), jnp.float32), g_bx, chan_start, 0
    )
    conv_b_grad = jnp.concatenate([bias_x_grad, g_bbc], 0)
    head_zeros = jnp.zeros((head_total,), jnp.float32)
    step_grad = lax.dynamic_update_slice_in_dim(head_zeros, g_step, head_start, 0)
    decay_grad = lax.dynamic_update_slice_in_dim(head_zeros, g_decay, head_start, 0)
    skip_grad = lax.dynamic_update_slice_in_dim(head_zeros, g_skip, head_start, 0)
    small_sums = lax.psum(
        (grad_pre, conv_w_grad, conv_b_grad, step_grad, decay_grad, skip_grad, grad_ngain),
        ("seq", "fsdp"),
    )
    fsdp_count = lax.axis_size("fsdp")
    fsdp_index = lax.axis_index("fsdp")
    in_width = normed.shape[1] // fsdp_count
    in_start = fsdp_index * in_width
    out_width = inner // fsdp_count
    out_start = fsdp_index * out_width
    normed_piece = lax.all_gather(normed, "fsdp", axis=0, tiled=True)
    proj_piece = lax.all_gather(proj_grad, "fsdp", axis=0, tiled=True)
    gate_piece = lax.all_gather(returned, "fsdp", axis=0, tiled=True)
    cot_piece = lax.all_gather(cot_half, "fsdp", axis=0, tiled=True)
    left = lax.dynamic_slice_in_dim(normed_piece, in_start, in_width, 1)
    right = lax.dynamic_slice_in_dim(gate_piece, out_start, out_width, 1)
    in_rows = jnp.dot(left.T, proj_piece, preferred_element_type=jnp.float32)
    out_rows = jnp.dot(right.T, cot_piece, preferred_element_type=jnp.float32)
    in_rows, out_rows = lax.psum((in_rows, out_rows), "seq")
    return (
        output[None],
        input_grad[None],
        in_rows,
        out_rows,
        small_sums[0],
        small_sums[1],
        small_sums[2],
        small_sums[3],
        small_sums[4],
        small_sums[5],
        small_sums[6],
    )


def solution(mesh):
    in_specs = (
        P("fsdp", "seq", None),
        P("fsdp", None),
        P(),
        P("fsdp", None),
        P(),
        P(),
        P(),
        P(),
        P(),
        P(),
        P("fsdp", None),
        P("fsdp", "seq", None),
    )
    out_specs = (
        P("fsdp", "seq", None),
        P("fsdp", "seq", None),
        P("fsdp", None),
        P("fsdp", None),
        P(),
        P(),
        P(),
        P(),
        P(),
        P(),
        P(),
    )
    return jax.shard_map(shards, mesh=mesh, in_specs=in_specs, out_specs=out_specs, check_vma=False)
```

profile of v0, /device:TPU:0, one launch (start us, length us, event | category | flops | bytes accessed | tf_op | source)
XLA Modules:
  0.0 1659.2 jit_solution(4961834603162615252)
XLA Ops:
  8.7 100.1 %all-gather.12.cloned.1.call-done = bf16[3072,1536]{1,0:T(8,128)(2,1)} async-done(((bf16[768,1536]{1,0:T(8,128)(2,1)}), bf16[3072,1536]{1,0:T(8,128)(2,1)}) %all-gather.12.cloned.1.call-update) | async-done | bytes 9437200 | tf_op jit(solution)/shard_map/all_gather | solution.py:129
  108.8 10.9 fusion.25
  119.7 7.8 copy.343
  128.0 16.7 %reduce.21 = bf16[3072,256]{1,0:T(8,128)(2,1)} reduce(bf16[3072,1,256]{2,1,0:T(2,128)(2,1)S(1)} %bitcast.391, bf16[]{:T(256)} %broadcast.367), dimensions={1}, to_apply=%bitcast.319.reduce_sub_computation | reduce | bytes 3145730
  154.3 139.8 %all-gather.10.cloned.1.call-done = bf16[1536,6448]{0,1:T(8,128)(2,1)} async-done(((bf16[384,6448]{0,1:T(8,128)(2,1)}), bf16[1536,6448]{0,1:T(8,128)(2,1)}) %all-gather.10.cloned.1.call-update) | async-done | bytes 19808272 | tf_op jit(solution)/shard_map/all_gather | solution.py:128
  294.0 9.8 convolution_convert_fusion
  313.8 20.6 %copy.314 = bf16[1,256,2,3072]{1,2,0,3:T(2,128)(2,1)} copy(bf16[1,256,2,3072]{1,3,2,0:T(8,128)(2,1)S(1)} %bitcast.399) | data formatting | bytes 6291456 | tf_op jit(solution)/shard_map/reshape | solution.py:136
  367.7 20.0 %all-gather.20.cloned.1.call-done = bf16[2048,256]{0,1:T(8,128)(2,1)} async-done(((bf16[256,256]{0,1:T(8,128)(2,1)}), bf16[2048,256]{0,1:T(8,128)(2,1)}) %all-gather.20.cloned.1.call-update) | async-done | bytes 1048592 | tf_op jit(solution)/shard_map/all_gather | solution.py:143
  401.3 18.8 %all-to-all-done = bf16[1,256,2,3072]{1,2,0,3:T(2,128)(2,1)} async-done(((bf16[1,256,2,3072]{1,2,0,3:T(2,128)(2,1)}), bf16[1,256,2,3072]{1,2,0,3:T(2,128)(2,1)}, u32[]{:S(2)}, u32[]{:S(2)}) %all-to-all-start) | async-done | bytes 3145760 | tf_op jit(solution)/shard_map/all_to_all | solution.py:139
  447.2 91.8 %while.34 = (s32[]{:T(128)}, f32[6,128,64]{2,1,0:T(8,128)}, f32[8,6,128,64]{3,2,1,0:T(8,128)}, f32[8,6,1,1]{1,3,2,0:T(1,128)}, f32[8,6,128,64]{2,3,1,0:T(8,128)}...) while((s32[]{:T(128)}, f32[6,128,64]{2,1,0:T(8,128)}, f32[8,6,128,64]{3,2,1,0:T(8,128)}, ...), condition=%wide.region_4.5_spmd.clone, body=%wide.region_3.4_spmd.clone.sunk | while | flops 196623 | bytes 2164440 | solution.py:86
  547.0 16.4 fusion.44
  572.2 15.5 psum.77
  592.7 14.6 psum.78
  622.0 14.9 fusion.12
  638.8 11.3 fusion.100
  658.1 83.1 %while.35 = (s32[]{:T(128)}, f32[6,128,64]{2,1,0:T(8,128)S(1)}, f32[8,6,128,64]{3,2,1,0:T(8,128)}, f32[8,6]{1,0:T(8,128)}, f32[8,6,128,64]{2,3,1,0:T(8,128)}, /*...) while((s32[]{:T(128)}, f32[6,128,64]{2,1,0:T(8,128)S(1)}, ...), condition=%wide.region_11.12_spmd.clone, body=%wide.region_9.11_spmd.clone.sunk | while | flops 294916 | bytes 2163056 | solution.py:86
  741.2 12.4 fusion.103
  785.8 35.5 %reduce.22 = bf16[2048,384]{1,0:T(8,128)(2,1)} reduce(bf16[2048,1,384]{2,1,0:T(2,128)(2,1)} %bitcast.394, bf16[]{:T(256)} %broadcast.367), dimensions={1}, to_apply=%bitcast.349.reduce_sub_computation | reduce | bytes 3145730
  825.1 42.3 %all_to_all.81 = bf16[8,2,49152]{2,1,0:T(2,128)(2,1)} all-to-all(bf16[8,2,49152]{2,1,0:T(2,128)(2,1)} %reshape.556), channel_id=1, replica_groups=mesh['seq'=8,'fsdp'=4] {'seq'}, dimensions={0} | all-to-all | bytes 3145728 | tf_op jit(solution)/shard_map/all_to_all | solution.py:170
  880.3 7.5 fusion.40
  897.2 14.9 reduce-window.16
  915.8 13.8 reduce.23
  935.4 11.9 bitcast_add_fusion.2
  955.9 8.3 multiply_reduce_fusion.5
  967.1 28.6 %copy.358 = bf16[1,2048,2,384]{3,2,0,1:T(2,128)(2,1)} copy(bf16[1,2048,2,384]{3,1,2,0:T(8,128)(2,1)S(1)} %maximum_bitcast_fusion) | data formatting | bytes 6291456 | tf_op jit(solution)/shard_map/broadcast_in_dim | solution.py:197
  1007.1 65.0 %all-to-all-done.4 = bf16[1,2048,2,384]{3,2,0,1:T(2,128)(2,1)S(1)} async-done(((bf16[1,2048,2,384]{3,2,0,1:T(2,128)(2,1)}), bf16[1,2048,2,384]{3,2,0,1:T(2,128)(2,1)S(1)}, u32[]{:S(2)}, u32[]{:S(2)}) %all-to-all-start.4) | async-done | bytes 3145760 | tf_op jit(solution)/shard_map/all_to_all | solution.py:199
  1087.3 16.3 fusion.82
  1111.1 95.4 %all-gather.16.cloned.1.call-done = bf16[1024,6448]{0,1:T(8,128)(2,1)} async-done(((bf16[256,6448]{0,1:T(8,128)(2,1)}), bf16[1024,6448]{0,1:T(8,128)(2,1)}) %all-gather.16.cloned.1.call-update) | async-done | bytes 13205520 | tf_op jit(solution)/shard_map/all_gather | solution.py:236
  1206.5 12.5 fusion.111
  1229.4 110.4 %all-reduce.28.cloned.1.call-done = (f32[1536]{0:T(1024)}, f32[4,3328]{1,0:T(4,128)}, f32[3328]{0:T(1024)}, f32[48]{0:T(128)}, f32[48]{0:T(128)}, /*index=5*/f32[48]{0:T(128)}, f32[3072]{0:T(1024)}) async-done(((f32[1536]{0:T(1024)}, f32[4,3328]{1,0:T(4,128)}, f32[3328]{0:T(1024)}, f32[48]{0:T(128)}, f32[48]{0:T(128)}, /*index=5*/f32[48]{0:T(128)}, f32[3072]{0:T(1024)}), (f32[1536]{0:T(1024)}, ...) | async-done | bytes 85584 | tf_op jit(solution)/shard_map/psum | solution.py:225
  1339.8 297.6 %all-reduce.30.cloned.1.call-done = (f32[384,6448]{0,1:T(8,128)}, f32[768,1536]{1,0:T(8,128)}) async-done(((f32[384,6448]{0,1:T(8,128)}, f32[768,1536]{1,0:T(8,128)}), (f32[384,6448]{0,1:T(8,128)}, f32[768,1536]{1,0:T(8,128)})) %all-reduce.30.cloned.1.call-update) | async-done | bytes 14622736 | tf_op jit(solution)/shard_map/psum | solution.py:243
  1637.4 8.5 copy.599
  (569 shorter events, 445.0 us)
Async XLA Ops:
  7.2 101.6 %copy-start.26 = (bf16[1,256,1536]{2,1,0:T(8,128)(2,1)S(1)}, bf16[1,256,1536]{2,1,0:T(8,128)(2,1)}, u32[]{:S(2)}) copy-start(bf16[1,256,1536]{2,1,0:T(8,128)(2,1)} %param.27) | copy-start | bytes 2359300
  7.2 101.6 %all-gather.12.cloned.1.call-start = ((), (), s32[]{:S(2)}) async-start(), calls=%async_computation.8 | async-start | bytes 11796480 | tf_op jit(solution)/shard_map/all_gather | solution.py:129
  7.9 286.1 %all-gather.10.cloned.1.call-start = ((), (), s32[]{:S(2)}) async-start(), calls=%async_computation.7 | async-start | bytes 24760320 | tf_op jit(solution)/shard_map/all_gather | solution.py:128
  148.5 158.5 %all-to-all-start.3 = ((bf16[8,2,49152]{2,1,0:T(2,128)(2,1)}), bf16[8,2,49152]{2,1,0:T(2,128)(2,1)S(1)}, u32[]{:S(2)}, u32[]{:S(2)}) async-start(bf16[8,2,49152]{2,1,0:T(2,128)(2,1)} %reshape.558), calls=%async_computation.3 | async-start | bytes 3145728 | tf_op jit(solution)/shard_map/all_to_all | solution.py:180
  154.2 149.6 %copy-start.28 = (bf16[256,1536]{1,0:T(8,128)(2,1)}, bf16[256,1536]{1,0:T(8,128)(2,1)S(1)}, u32[]{:S(2)}) copy-start(bf16[256,1536]{1,0:T(8,128)(2,1)S(1)} %fusion.76) | copy-start | bytes 2359300
  307.1 27.4 %all-to-all-start.1 = ((bf16[8,2,768]{2,1,0:T(2,128)(2,1)}), bf16[8,2,768]{2,1,0:T(2,128)(2,1)S(1)}, u32[]{:S(2)}, u32[]{:S(2)}) async-start(bf16[8,2,768]{2,1,0:T(2,128)(2,1)} %reshape.554), calls=%async_computation.1 | async-start | bytes 49152 | tf_op jit(solution)/shard_map/all_to_all | solution.py:140
  335.0 85.1 %all-to-all-start = ((bf16[1,256,2,3072]{1,2,0,3:T(2,128)(2,1)}), bf16[1,256,2,3072]{1,2,0,3:T(2,128)(2,1)}, u32[]{:S(2)}, u32[]{:S(2)}) async-start(bf16[1,256,2,3072]{1,2,0,3:T(2,128)(2,1)} %copy.314), calls=%async_computation | async-start | bytes 6291456 | tf_op jit(solution)/shard_map/all_to_all | solution.py:139
  340.1 47.6 %all-gather.20.cloned.1.call-start = ((), (), s32[]{:S(2)}) async-start(), calls=%async_computation.13 | async-start | bytes 1179648 | tf_op jit(solution)/shard_map/all_gather | solution.py:143
  349.9 656.2 %reduce-scatter.2.cloned.1.call-start = ((), (), s32[]{:S(2)}) async-start(), calls=%async_computation.9 | async-start | bytes 2359296 | tf_op jit(solution)/shard_map/reduce_scatter | solution.py:202
  359.9 29.3 %copy-start.46 = (f32[2048]{0:T(1024)S(1)}, f32[2048]{0:T(1024)}, u32[]{:S(2)}) copy-start(f32[2048]{0:T(1024)} %get-tuple-element.453) | copy-start | bytes 24580
  359.9 29.3 %slice-start.1 = ((f32[3328]{0:T(1024)}), f32[256]{0:T(256)S(1)}, s32[]{:S(2)}) async-start(f32[3328]{0:T(1024)} %param.21), calls=%async_computation.18 | async-start | bytes 2048 | tf_op jit(solution)/shard_map/slice | solution.py:153
  359.9 29.4 %copy-start.89 = (f32[1,256]{1,0:T(1,128)S(1)}, f32[1,256]{1,0:T(1,128)}, u32[]{:S(2)}) copy-start(f32[1,256]{1,0:T(1,128)} %get-tuple-element.440) | copy-start | bytes 3076
  359.9 29.4 %copy-start.91 = (f32[1,256]{1,0:T(1,128)S(1)}, f32[1,256]{1,0:T(1,128)}, u32[]{:S(2)}) copy-start(f32[1,256]{1,0:T(1,128)} %get-tuple-element.441) | copy-start | bytes 3076
  359.9 29.4 %copy-start.93 = (f32[1,256]{1,0:T(1,128)S(1)}, f32[1,256]{1,0:T(1,128)}, u32[]{:S(2)}) copy-start(f32[1,256]{1,0:T(1,128)} %get-tuple-element.442) | copy-start | bytes 3076
  359.9 29.4 %copy-start.95 = (f32[1,256]{1,0:T(1,128)S(1)}, f32[1,256]{1,0:T(1,128)}, u32[]{:S(2)}) copy-start(f32[1,256]{1,0:T(1,128)} %get-tuple-element.443) | copy-start | bytes 3076
  360.7 31.7 %copy-start.29 = (f32[1,8,256,1,6]{2,3,4,1,0:T(1,128)}, f32[1,8,256,1,6]{2,3,4,1,0:T(1,128)S(1)}, u32[]{:S(2)}) copy-start(f32[1,8,256,1,6]{2,3,4,1,0:T(1,128)S(1)} %convert_bitcast_fusion.2) | copy-start | bytes 147460
  365.4 27.0 %copy-start.56 = (f32[8,6,256]{2,1,0:T(8,128)}, f32[8,6,256]{2,1,0:T(8,128)S(1)}, u32[]{:S(2)}) copy-start(f32[8,6,256]{2,1,0:T(8,128)S(1)} %copy.541) | copy-start | bytes 147460
  365.6 26.9 %copy-start.53 = (f32[8,6]{1,0:T(8,128)}, f32[8,6]{1,0:T(8,128)S(1)}, u32[]{:S(2)}) copy-start(f32[8,6]{1,0:T(8,128)S(1)} %slice_reduce_fusion) | copy-start | bytes 580
  398.1 26.0 %copy-start.18 = (f32[8,256,128]{2,1,0:T(8,128)}, f32[8,256,128]{2,1,0:T(8,128)S(1)}, u32[]{:S(2)}) copy-start(f32[8,256,128]{2,1,0:T(8,128)S(1)} %copy.319) | copy-start | bytes 3145732
  779.3 324.6 %all-gather.22.cloned.1.call-start = ((), (), s32[]{:S(2)}) async-start(), calls=%async_computation.14 | async-start | bytes 3932160 | tf_op jit(solution)/shard_map/all_gather | solution.py:238
  779.9 324.0 %all-gather.18.cloned.1.call-start = ((), (), s32[]{:S(2)}) async-start(), calls=%async_computation.12 | async-start | bytes 7864320 | tf_op jit(solution)/shard_map/all_gather | solution.py:237
  891.6 21.9 %copy-start.50 = (f32[1,2048,1,6]{1,3,2,0:T(8,128)S(1)}, f32[1,2048,1,6]{1,3,2,0:T(8,128)}, u32[]{:S(2)}) copy-start(f32[1,2048,1,6]{1,3,2,0:T(8,128)} %reshape.539) | copy-start | bytes 147460
  895.9 39.4 %copy-start.1 = (f32[48,8,8,256]{3,2,1,0:T(8,128)S(1)}, f32[48,8,8,256]{3,2,1,0:T(8,128)}, u32[]{:S(2)}) copy-start(f32[48,8,8,256]{3,2,1,0:T(8,128)} %copy-done) | copy-start | bytes 9437188
  895.9 39.4 %copy-start.41 = (f32[8,256,6]{1,2,0:T(8,128)S(1)}, f32[8,256,6]{1,2,0:T(8,128)}, u32[]{:S(2)}) copy-start(f32[8,256,6]{1,2,0:T(8,128)} %get-tuple-element.445) | copy-start | bytes 147460
  913.5 21.8 %copy-start.59 = (f32[8,6,256]{2,1,0:T(8,128)S(1)}, f32[8,6,256]{2,1,0:T(8,128)}, u32[]{:S(2)}) copy-start(f32[8,6,256]{2,1,0:T(8,128)} %copy-done.56) | copy-start | bytes 147460
  913.7 21.7 %copy-start.67 = (f32[8,256,6]{1,2,0:T(8,128)S(1)}, f32[8,256,6]{1,2,0:T(8,128)}, u32[]{:S(2)}) copy-start(f32[8,256,6]{1,2,0:T(8,128)} %get-tuple-element.444) | copy-start | bytes 147460
  932.0 63.7 %all-to-all-start.5 = ((bf16[8,2,768]{2,1,0:T(2,128)(2,1)}), bf16[8,2,768]{2,1,0:T(2,128)(2,1)S(1)}, u32[]{:S(2)}, u32[]{:S(2)}) async-start(bf16[8,2,768]{2,1,0:T(2,128)(2,1)} %reshape.560), calls=%async_computation.6 | async-start | bytes 49152 | tf_op jit(solution)/shard_map/all_to_all | solution.py:200
  995.6 76.5 %all-to-all-start.4 = ((bf16[1,2048,2,384]{3,2,0,1:T(2,128)(2,1)}), bf16[1,2048,2,384]{3,2,0,1:T(2,128)(2,1)S(1)}, u32[]{:S(2)}, u32[]{:S(2)}) async-start(bf16[1,2048,2,384]{3,2,0,1:T(2,128)(2,1)} %copy.358), calls=%async_computation.4 | async-start | bytes 6291456 | tf_op jit(solution)/shard_map/all_to_all | solution.py:199
  1000.7 110.4 %all-gather.14.cloned.1.call-start = ((), (), s32[]{:S(2)}) async-start(), calls=%async_computation.10 | async-start | bytes 3932160 | tf_op jit(solution)/shard_map/all_gather | solution.py:235
  1001.4 205.1 %all-gather.16.cloned.1.call-start = ((), (), s32[]{:S(2)}) async-start(), calls=%async_computation.11 | async-start | bytes 16506880 | tf_op jit(solution)/shard_map/all_gather | solution.py:236
  1081.0 258.8 %all-reduce.28.cloned.1.call-start = ((), (), s32[]{:S(2)}) async-start(), calls=%async_computation.15 | async-start | bytes 183296 | tf_op jit(solution)/shard_map/psum | solution.py:225
  1103.6 533.8 %all-reduce.30.cloned.1.call-start = ((), (), s32[]{:S(2)}) async-start(), calls=%async_computation.16 | async-start | bytes 29245440 | tf_op jit(solution)/shard_map/psum | solution.py:243
  (105 other events, 603.3 us)
Sparse Core Ops, SparseCore 0:
  9.8 98.9 all-gather.11
  110.6 183.3 all-gather.9
  350.1 37.6 all-gather.19
  779.4 33.2 reduce-scatter.1
  814.4 42.4 all-gather.21
  879.8 67.7 all-gather.17
  1003.9 44.3 all-gather.13
  1081.0 125.4 all-gather.15
  1214.1 125.6 all-reduce.27
  1342.7 294.7 all-reduce.29
where the time goes:
time: 1670 us; the launch traced here: 1660 us
  waiting for transfers between devices  850 us (51%)
  local copies, waits for them, and re-layouts  295 us (18%)
  other arithmetic  236 us (14%)
  matrix products  166 us (10%)
  blocking collectives  72.3 us (4%)
  starting transfers between devices  23.8 us (1%)
    psum x1, waiting for transfers between devices, shards(): in_rows, out_rows = lax.psum((in_rows, out_rows), 'seq')  298 us
    all_gather x1, waiting for transfers between devices, shards(): lax.all_gather(w_in, 'fsdp', axis=0, tiled=True)  140 us
    psum x1, waiting for transfers between devices, shards(): lax.psum((grad_pre, conv_w_grad, conv_b_grad, step_grad, decay_grad, skip...  110 us
    all_gather x1, waiting for transfers between devices, shards(): lax.all_gather(w_out, 'fsdp', axis=0, tiled=True)  100 us
    all_gather x1, waiting for transfers between devices, shards(): proj_piece = lax.all_gather(proj_grad, 'fsdp', axis=0, tiled=True)  95.4 us
    dynamic_slice x48, local copies, waits for them, and re-layouts, mixer(): lax.scan(carry_step, jnp.zeros((head_count, N, P_SIZE), jnp.float32), (st...  74.8 us
    unnamed x8, other arithmetic  69.4 us
    unnamed x270, local copies, waits for them, and re-layouts  67.6 us
  transfers between devices with their start and end apart: 15, of which 8 were waited for; matrix products, arithmetic and copies ran while one was open for 21% of the time, Pallas kernels for 0%

commit v1 on v0

v1 whole, which is shorter than its diff:
```python
import functools

import jax
import jax.numpy as jnp
from jax import lax
from jax.experimental import pallas as pl
from jax.experimental.pallas import tpu as pltpu
from jax.sharding import PartitionSpec as P

P_SIZE = 64
N = 128
TAPS = 4
HALO = TAPS - 1
EDGE = 8
LANES = 128
EPSILON = 1e-05
F32 = jnp.float32
BF16 = jnp.bfloat16
MESH = pl.DeviceIdType.MESH
ANY = pl.BlockSpec(memory_space=pl.ANY)
VMEM = pl.BlockSpec(memory_space=pltpu.VMEM)
VMEM_BYTES = 56 << 20


def half(value):
    return value.astype(BF16)


def mm(left, right, dims):
    return lax.dot_general(half(left), half(right), (dims, ((), ())), preferred_element_type=F32)


NN = ((1,), (0,))
NT = ((1,), (1,))
TN = ((0,), (0,))


def split_dot(value, table, dims):
    top = half(value)
    rest = half(value - top.astype(F32))
    return mm(top, table, dims) + mm(rest, table, dims)


def head_table(channels):
    row = lax.broadcasted_iota(jnp.int32, (LANES, channels), 0)
    col = lax.broadcasted_iota(jnp.int32, (LANES, channels), 1)
    low = row * P_SIZE
    return half(((col >= low) & (col < low + P_SIZE)).astype(F32))


def triangle(length, lower):
    row = lax.broadcasted_iota(jnp.int32, (length, length), 0)
    col = lax.broadcasted_iota(jnp.int32, (length, length), 1)
    return half(((row >= col) if lower else (row <= col)).astype(F32))


def running_sum(values, lower):
    table = triangle(values.shape[0], lower)
    a = half(values)
    rest = values - a.astype(F32)
    b = half(rest)
    c = half(rest - b.astype(F32))
    return mm(table, a, NN) + mm(table, b, NN) + mm(table, c, NN)


def softplus(value):
    return jnp.maximum(value, 0.0) + jnp.log1p(jnp.exp(-jnp.abs(value)))


def params(**more):
    return pltpu.CompilerParams(vmem_limit_bytes=VMEM_BYTES, **more)


def meet(targets):
    barrier = pltpu.get_barrier_semaphore()
    for target in targets:
        pl.semaphore_signal(barrier, inc=1, device_id=target, device_id_type=MESH)
    pl.semaphore_wait(barrier, len(targets))


def remote(src, dst, send, recv, target):
    return pltpu.make_async_remote_copy(
        src_ref=src, dst_ref=dst, send_sem=send, recv_sem=recv, device_id=target, device_id_type=MESH
    )


def gather_kernel(n_s, n_f, C, DI, tok, seg, w, tok_all, seg_all, w_z, w_x, w_b, edge, edge_own, b_tok, b_z, b_x, b_b, b_seg, snd, rcv, loc):
    s, f = lax.axis_index("seq"), lax.axis_index("fsdp")
    L, R = tok.shape[0], w.shape[0]
    tail = w.shape[1] - 2 * DI
    right, left = lax.rem(s + 1, n_s), lax.rem(s + n_s - 1, n_s)
    parity = lax.rem(s, 2)
    pair = s + 1 - 2 * parity
    peers = [lax.rem(f + k, n_f) for k in range(1, n_f)]
    meet([(right, f), (left, f)] + [(s, p) for p in peers])
    count = [0]

    def go(src, dst, target):
        i = count[0]
        count[0] = i + 1
        copy = remote(src, dst, snd.at[i], rcv.at[i], target)
        copy.start()
        return copy

    halves = pl.ds(pl.multiple_of(parity * (R // 2), R // 2), R // 2)
    others = pl.ds(pl.multiple_of((1 - parity) * (R // 2), R // 2), R // 2)
    cols = [pl.ds(pl.multiple_of(p * C, C), C) for p in range(2 * n_f)]

    def part(j, base):
        return pl.ds(pl.multiple_of(base + j * C, C), C)

    first = go(tok.at[pl.ds(L - EDGE, EDGE)], edge_own, (right, f))
    started = []
    for p in peers:
        started.append(go(seg, seg_all.at[f], (s, p)))
        started.append(go(tok, tok_all.at[f], (s, p)))
    w_copies = []
    for p in peers:
        w_copies.append(
            [
                go(w.at[halves, part(p, 0)], w_z.at[f, halves], (s, p)),
                go(w.at[halves, part(p, DI)], w_x.at[f, halves], (s, p)),
                go(w.at[halves, pl.ds(2 * DI, tail)], w_b.at[f, halves], (s, p)),
            ]
        )
    mine = [
        (tok, b_tok, tok_all.at[f]),
        (seg, b_seg, seg_all.at[f]),
        (w.at[:, part(f, 0)], b_z, w_z.at[f]),
        (w.at[:, part(f, DI)], b_x, w_x.at[f]),
        (w.at[:, pl.ds(2 * DI, tail)], b_b, w_b.at[f]),
    ]
    ins = [pltpu.make_async_copy(a, b, loc.at[i]) for i, (a, b, _) in enumerate(mine)]
    for c in ins:
        c.start()
    first.wait()
    edges = [go(edge_own, edge.at[f], (s, p)) for p in peers]
    own_edge = pltpu.make_async_copy(edge_own, edge.at[f], loc.at[len(mine)])
    own_edge.start()
    outs = []
    for i, (_, b, c) in enumerate(mine):
        ins[i].wait()
        out = pltpu.make_async_copy(b, c, loc.at[len(mine) + 1 + i])
        out.start()
        outs.append(out)
    relays = []
    for k, copies in enumerate(w_copies):
        source = lax.rem(f + n_f - (k + 1), n_f)
        for copy, array in zip(copies, (w_z, w_x, w_b)):
            copy.wait_recv()
            relays.append(go(array.at[source, halves], array.at[source, halves], (pair, f)))
    for copy in relays:
        copy.wait()
    for copies in w_copies:
        for copy in copies:
            copy.wait_send()
    for copy in started + edges:
        copy.wait()
    own_edge.wait()
    for out in outs:
        out.wait()


def gather(tok, seg, w, C, DI, n_s, n_f):
    L, D = tok.shape
    R = w.shape[0]
    tail = w.shape[1] - 2 * DI
    copies = 1 + 6 * (n_f - 1) + 3 * (n_f - 1)
    sems = copies
    outs = [
        jax.ShapeDtypeStruct((n_f, L, D), BF16),
        jax.ShapeDtypeStruct((n_f,) + seg.shape, seg.dtype),
        jax.ShapeDtypeStruct((n_f, R, C), BF16),
        jax.ShapeDtypeStruct((n_f, R, C), BF16),
        jax.ShapeDtypeStruct((n_f, R, tail), BF16),
        jax.ShapeDtypeStruct((n_f, EDGE, D), BF16),
        jax.ShapeDtypeStruct((EDGE, D), BF16),
    ]
    return pl.pallas_call(
        functools.partial(gather_kernel, n_s, n_f, C, DI),
        name="gather",
        out_shape=outs,
        in_specs=[ANY] * 3,
        out_specs=[ANY] * 7,
        scratch_shapes=[
            pltpu.VMEM((L, D), BF16),
            pltpu.VMEM((R, C), BF16),
            pltpu.VMEM((R, C), BF16),
            pltpu.VMEM((R, tail), BF16),
            pltpu.VMEM(seg.shape, seg.dtype),
            pltpu.SemaphoreType.DMA((sems,)),
            pltpu.SemaphoreType.DMA((sems,)),
            pltpu.SemaphoreType.DMA((11,)),
        ],
        compiler_params=params(collective_id=0, has_side_effects=True),
    )(tok, seg, w)


def chain_kernel(n_s, forward, state, through, result, out, snd, rcv):
    s, f = lax.axis_index("seq"), lax.axis_index("fsdp")
    right, left = lax.rem(s + 1, n_s), lax.rem(s + n_s - 1, n_s)
    meet([(right, f), (left, f)])
    target = right if forward else left
    first = s == (0 if forward else n_s - 1)
    last = s == (n_s - 1 if forward else 0)
    copies = []
    for q in range(state.shape[0]):
        copy = remote(out.at[q], result.at[q], snd.at[q], rcv.at[q], (target, f))
        copies.append(copy)

        @pl.when(first)
        def _():
            result[q] = jnp.zeros_like(result[q])

        @pl.when(jnp.logical_not(first))
        def _():
            copy.wait_recv()

        out[q] = half(state[q] + result[q].astype(F32) * through[q, 0:1, :])

        @pl.when(jnp.logical_not(last))
        def _():
            copy.start()

    @pl.when(jnp.logical_not(last))
    def _():
        for copy in copies:
            copy.wait_send()


def chain(states, through, forward, n_s):
    return pl.pallas_call(
        functools.partial(chain_kernel, n_s, forward),
        name="chain_on" if forward else "chain_back",
        out_shape=jax.ShapeDtypeStruct(states.shape, BF16),
        in_specs=[VMEM] * 2,
        out_specs=VMEM,
        scratch_shapes=[
            pltpu.VMEM(states.shape, BF16),
            pltpu.SemaphoreType.DMA((states.shape[0],)),
            pltpu.SemaphoreType.DMA((states.shape[0],)),
        ],
        compiler_params=params(collective_id=1 if forward else 2, has_side_effects=True),
    )(states, through)


def total_kernel(n_f, part, total, got, snd, rcv):
    s, f = lax.axis_index("seq"), lax.axis_index("fsdp")
    peers = [lax.rem(f + k, n_f) for k in range(1, n_f)]
    meet([(s, p) for p in peers])
    copies = []
    for k, p in enumerate(peers):
        copy = remote(part, got.at[k], snd.at[k], rcv.at[k], (s, p))
        copy.start()
        copies.append(copy)
    value = part[...]
    for k, copy in enumerate(copies):
        copy.wait()
        value = value + got[k]
    total[...] = value


def total_over_fsdp(part, n_f):
    return pl.pallas_call(
        functools.partial(total_kernel, n_f),
        name="total",
        out_shape=jax.ShapeDtypeStruct(part.shape, F32),
        in_specs=[VMEM],
        out_specs=VMEM,
        scratch_shapes=[
            pltpu.VMEM((n_f - 1,) + part.shape, F32),
            pltpu.SemaphoreType.DMA((n_f - 1,)),
            pltpu.SemaphoreType.DMA((n_f - 1,)),
        ],
        compiler_params=params(collective_id=3, has_side_effects=True),
    )(part)


def fill(scratch, halo, raw):
    length = raw.shape[0]
    scratch[0:EDGE, :] = halo.astype(F32)
    scratch[EDGE : EDGE + length, :] = raw.astype(F32)


def conv(scratch, length, kernel, cols):
    pre = kernel[TAPS : TAPS + 1, :] + kernel[HALO : HALO + 1, :] * scratch[EDGE : EDGE + length, :]
    for k in range(HALO):
        start = EDGE - HALO + k
        pre = pre + kernel[k : k + 1, :] * (scratch[start : start + length, :] * cols[:, k : k + 1])
    return pre


def silu(value):
    return value * jax.nn.sigmoid(value)


def enter_kernel(x, x_halo, b, b_halo, d, cols, k_x, k_b, heads, state, through, pre_x, xd, pre_b, bc, cum, cum_row, s_x, s_b):
    L, C = x.shape
    table = head_table(C)
    c = cols[...]
    fill(s_x, x_halo[...], x[...])
    fill(s_b, b_halo[...], b[...])
    px = conv(s_x, L, k_x, c)
    pb = conv(s_b, L, k_b, c)
    pre_x[...] = px
    pre_b[...] = pb
    bc[...] = half(silu(pb))
    step = softplus(d[...].astype(F32) + heads[0:1, :])
    rate = -step * heads[1:2, :]
    total = running_sum(rate, True)
    cum[...] = total
    cum_row[...] = jnp.transpose(total)[0 : cum_row.shape[0], :]
    last = total[L - 1 : L, :]
    to_end = jnp.exp(last - total) * c[:, 3:4]
    entry_last = jnp.exp(last) * c[L - 1 : L, 4:5]
    through[...] = split_dot(jnp.broadcast_to(entry_last, (8, LANES)), table, NN)
    xdv = split_dot(step, table, NN) * silu(px)
    xd[...] = half(xdv)
    wx = half(split_dot(to_end, table, NN) * xdv)
    state[...] = mm(bc[:, 0:N], wx, TN)


def block_rows(L):
    return min(L, 128)


def live_rows(cols, seg_row, r, rows, width):
    row = lax.broadcasted_iota(jnp.int32, (rows, width), 0) + r * rows
    col = lax.broadcasted_iota(jnp.int32, (rows, width), 1)
    same = cols[r * rows : (r + 1) * rows, 5:6] == seg_row[0:1, 0:width]
    return (row >= col) & same


def mix_kernel(pre_x, xd, bc, cum, cum_row, cols, seg_row, enter, z, gg, gain, heads, plain, mixed, sums):
    L, C = xd.shape
    rows = block_rows(L)
    table = head_table(C)
    cv = cum[...]
    entry = jnp.exp(cv) * cols[:, 4:5]
    carried = mm(bc[:, N : 2 * N], enter[...], NN) * split_dot(entry, table, NN)
    for r in range(L // rows):
        width = (r + 1) * rows
        mine = slice(r * rows, (r + 1) * rows)
        scores = jnp.where(
            live_rows(cols, seg_row, r, rows, width), mm(bc[mine, N : 2 * N], bc[0:width, 0:N], NT), 0.0
        )
        for h in range(0, C // P_SIZE, 2):
            pieces = []
            for g in (h, h + 1):
                gap = jnp.minimum(cum[mine, g : g + 1] - cum_row[g : g + 1, 0:width], 0.0)
                pieces.append(mm(scores * jnp.exp(gap), xd[0:width, g * P_SIZE : (g + 1) * P_SIZE], NN))
            plain[mine, h * P_SIZE : (h + 2) * P_SIZE] = jnp.concatenate(pieces, 1)
    y = plain[...] + carried
    plain[...] = y
    skip = split_dot(jnp.broadcast_to(heads[2:3, :], (8, LANES)), table, NN)[0:1, :]
    m = half(y + skip * silu(pre_x[...]))
    mixed[...] = m
    gated = m.astype(F32) * silu(z[...].astype(F32))
    sg = gg[...].astype(F32) * gain[0:1, :]
    one = jnp.sum(gated * gated, 1, keepdims=True)
    two = jnp.sum(sg * gated, 1, keepdims=True)
    lane = lax.broadcasted_iota(jnp.int32, (L, LANES), 1)
    both = jnp.where(lane == 0, one, jnp.where(lane == 1, two, 0.0))
    sums[...] = jnp.transpose(both)[0:8, :]


def gate_kernel(DI, mixed, z, gg, gain, total, cum, cols, bc, ngate, dz, dy, d_enter, d_gain):
    L, C = mixed.shape
    table = head_table(C)
    sums = jnp.transpose(jnp.concatenate([total[...], jnp.zeros((LANES - 8, L), F32)], 0))
    inv = lax.rsqrt(sums[:, 0:1] / DI + EPSILON)
    inner = inv * (sums[:, 1:2] / DI)
    y = mixed[...].astype(F32)
    zf = z[...].astype(F32)
    sig = jax.nn.sigmoid(zf)
    gz = zf * sig
    unit = y * gz * inv
    g = gg[...].astype(F32)
    ngate[...] = half(unit * gain[0:1, :])

    @pl.when(pl.program_id(0) == 0)
    def _():
        d_gain[...] = jnp.zeros_like(d_gain)

    d_gain[...] += jnp.broadcast_to(jnp.sum(g * unit, 0, keepdims=True), d_gain.shape)
    grad = inv * (g * gain[0:1, :] - unit * inner)
    d = half(grad * gz)
    dy[...] = d
    dz[...] = half(grad * y * sig * (1.0 + zf * (1.0 - sig)))
    entry = jnp.exp(cum[...]) * cols[:, 4:5]
    edy = half(split_dot(entry, table, NN) * d.astype(F32))
    d_enter[...] = mm(bc[:, N : 2 * N], edy, TN)


def silu_grad(pre, sigma):
    return sigma * (1.0 + pre * (1.0 - sigma))


def conv_back(dpre, raw, halo, kernel, cols, s_raw, s_grad, grads):
    length = dpre.shape[0]
    fill(s_raw, halo, raw)
    grads[TAPS : TAPS + 1, :] += jnp.sum(dpre, 0, keepdims=True)
    grads[HALO : HALO + 1, :] += jnp.sum(dpre * s_raw[EDGE : EDGE + length, :], 0, keepdims=True)
    d_raw = kernel[HALO : HALO + 1, :] * dpre
    width = dpre.shape[1]
    d_halo = jnp.zeros((EDGE, width), F32)
    s_grad[0:EDGE, :] = jnp.zeros((EDGE, width), F32)
    s_grad[EDGE + length : EDGE + length + EDGE, :] = jnp.zeros((EDGE, width), F32)
    for k in range(HALO):
        masked = dpre * cols[:, k : k + 1]
        start = EDGE - HALO + k
        grads[k : k + 1, :] += jnp.sum(masked * s_raw[start : start + length, :], 0, keepdims=True)
        s_grad[EDGE : EDGE + length, :] = masked
        up = HALO - k
        d_raw = d_raw + kernel[k : k + 1, :] * s_grad[EDGE + up : EDGE + up + length, :]
        d_halo = d_halo + kernel[k : k + 1, :] * s_grad[up : up + EDGE, :]
    return d_raw, d_halo


def back_kernel(
    x, x_halo, b, b_halo, d, cols, seg_row, k_x, k_b, heads, pre_x, xd, pre_b, bc, cum, cum_row, enter, grad, plain, dy,
    dx, db, dd, tail, halo, g_x, g_b, g_h, s_x, s_gx, s_b, s_gb, s_dxd, s_ds,
):
    L, C = xd.shape
    rows = block_rows(L)
    table = head_table(C)
    c = cols[...]
    cv = cum[...]

    @pl.when(pl.program_id(0) == 0)
    def _():
        g_x[...] = jnp.zeros_like(g_x)
        g_b[...] = jnp.zeros_like(g_b)
        g_h[...] = jnp.zeros_like(g_h)

    s_dxd[...] = jnp.zeros_like(s_dxd)
    s_ds[...] = jnp.zeros_like(s_ds)
    for r in range(L // rows):
        width = (r + 1) * rows
        mine = slice(r * rows, (r + 1) * rows)
        live = live_rows(cols, seg_row, r, rows, width)
        scores = jnp.where(live, mm(bc[mine, N : 2 * N], bc[0:width, 0:N], NT), 0.0)
        d_scores = jnp.zeros((rows, width), F32)
        for h in range(0, C // P_SIZE, 2):
            pieces = []
            for g in (h, h + 1):
                lanes = slice(g * P_SIZE, (g + 1) * P_SIZE)
                decay = jnp.exp(jnp.minimum(cum[mine, g : g + 1] - cum_row[g : g + 1, 0:width], 0.0))
                pieces.append(mm(scores * decay, dy[mine, lanes], TN))
                d_scores = d_scores + mm(dy[mine, lanes], xd[0:width, lanes], NT) * decay
            s_dxd[0:width, h * P_SIZE : (h + 2) * P_SIZE] += jnp.concatenate(pieces, 1)
        s_ds[mine, 0:width] = jnp.where(live, d_scores, 0.0)
    ds = half(s_ds[...])
    last = cv[L - 1 : L, :]
    to_end = split_dot(jnp.exp(last - cv) * c[:, 3:4], table, NN)
    entry = split_dot(jnp.exp(cv) * c[:, 4:5], table, NN)
    dyf = dy[...].astype(F32)
    xdf = xd[...].astype(F32)
    dwx = mm(bc[:, 0:N], grad[...], NN)
    wx = half(to_end * xdf)
    d_b = mm(wx, grad[...], NT) + mm(ds, bc[:, N : 2 * N], TN)
    d_c = mm(half(entry * dyf), enter[...], NT) + mm(ds, bc[:, 0:N], NN)
    u = split_dot(wx.astype(F32) * dwx, table, NT)
    dxd_in = s_dxd[...]
    dcum = split_dot(dyf * plain[...] - xdf * dxd_in, table, NT) - u
    carry = jnp.sum(enter[...].astype(F32) * grad[...].astype(F32), 0, keepdims=True)
    carry = split_dot(jnp.broadcast_to(carry, (8, C)), table, NT)[0:1, :]
    at_last = jnp.sum(u, 0, keepdims=True) + jnp.exp(last) * c[L - 1 : L, 4:5] * carry
    row = lax.broadcasted_iota(jnp.int32, (L, LANES), 0)
    dcum = dcum + jnp.where(row == L - 1, at_last, 0.0)
    drate = running_sum(dcum, False)
    px = pre_x[...]
    sig = jax.nn.sigmoid(px)
    xf = px * sig
    dxd = dxd_in + to_end * dwx
    raw_step = d[...].astype(F32) + heads[0:1, :]
    step = softplus(raw_step)
    ddt = split_dot(xf * dxd, table, NT) - drate * heads[1:2, :]
    ddt_raw = ddt * jax.nn.sigmoid(raw_step)
    dd[...] = half(ddt_raw)
    g_h[0:1, :] += jnp.sum(ddt_raw, 0, keepdims=True)
    g_h[1:2, :] += jnp.sum(drate * (-step * heads[1:2, :]), 0, keepdims=True)
    g_h[2:3, :] += split_dot(jnp.broadcast_to(jnp.sum(dyf * xf, 0, keepdims=True), (8, C)), table, NT)[0:1, :]
    skip = split_dot(jnp.broadcast_to(heads[2:3, :], (8, LANES)), table, NN)[0:1, :]
    d_x = split_dot(step, table, NN) * dxd + skip * dyf
    rx, hx = conv_back(d_x * silu_grad(px, sig), x[...], x_halo[...], k_x, c, s_x, s_gx, g_x)
    pb = pre_b[...]
    d_bc = jnp.concatenate([d_b, d_c], 1) * silu_grad(pb, jax.nn.sigmoid(pb))
    rb, hb = conv_back(d_bc, b[...], b_halo[...], k_b, c, s_b, s_gb, g_b)
    dx[...] = half(rx)
    db[...] = half(rb)
    tail[:, 0:C] = rx[L - EDGE : L, :]
    tail[:, C : C + 2 * N] = rb[L - EDGE : L, :]
    halo[:, 0:C] = half(hx)
    halo[:, C : C + 2 * N] = half(hb)


def per(*shape, col=0):
    return pl.BlockSpec((None,) + shape, lambda q: (q, 0, col))


def fixed(*shape):
    return pl.BlockSpec(shape, lambda q: (0,) * len(shape))


def shaped(*shape, dtype=F32):
    return jax.ShapeDtypeStruct(shape, dtype)


def shards(tokens, seg_ids, pre_gain, w_in, conv_weight, conv_bias, dt_bias, a_log, d_skip, norm_gain, w_out, cotangent):
    n_s = lax.axis_size("seq")
    n_f = lax.axis_size("fsdp")
    s = lax.axis_index("seq")
    f = lax.axis_index("fsdp")
    L, D = tokens.shape[1:]
    DI = norm_gain.shape[0]
    H = dt_bias.shape[0]
    Hl = H // n_f
    C = DI // n_f
    pair = conv_bias.shape[0] - DI
    T = n_f * L
    rows = w_in.shape[0]
    HR = -(-Hl // 8) * 8

    def mine(array, width, axis):
        return lax.dynamic_slice_in_dim(array, f * width, width, axis)

    tok_all, seg_full, w_z, w_x, w_b, edge, _ = gather(tokens[0], seg_ids, w_in, C, DI, n_s, n_f)
    w_z, w_x, w_b = w_z.reshape(D, C), w_x.reshape(D, C), w_b.reshape(D, pair + H)
    cot_own, _ = lax.optimization_barrier((cotangent[0], tok_all))
    cot_all = lax.all_gather(cot_own, "fsdp").reshape(T, D)
    seg_full = seg_full[:, 0]
    seg_pad = jnp.pad(seg_full, ((0, 0), (HALO, 0)), constant_values=-1)
    seg_ext = lax.dynamic_slice_in_dim(seg_pad, s * L, L + HALO, 1)
    seg = seg_ext[:, HALO:]
    marks = [seg_ext[:, k : k + L] == seg for k in range(HALO)]
    marks += [seg == seg[:, L - 1 :], seg == seg_ext[:, HALO - 1 : HALO], seg]
    cols = jnp.stack([m.astype(F32) for m in marks] + [jnp.zeros_like(seg, F32)] * (LANES - len(marks)), -1)
    seg_row = jnp.broadcast_to(seg.astype(F32)[:, None, :], (n_f, 8, L))

    def norm(values):
        values = values.astype(F32)
        inv = lax.rsqrt(jnp.mean(values * values, -1, keepdims=True) + EPSILON)
        return half(values * inv * pre_gain)

    normed = norm(tok_all).reshape(T, D)
    normed_edge = norm(edge).reshape(n_f * EDGE, D)

    def dot(a, b):
        return jnp.dot(a, b, preferred_element_type=F32)

    def dot_t(a, b):
        return lax.dot_general(a, b, (((1,), (1,)), ((), ())), preferred_element_type=F32)

    def t_dot(a, b):
        return lax.dot_general(a, b, (((0,), (0,)), ((), ())), preferred_element_type=F32)

    def lanes_of(values):
        return jnp.pad(mine(values, Hl, values.ndim - 1), ((0, 0),) * (values.ndim - 1) + ((0, LANES - Hl),))

    z = half(dot(normed, w_z)).reshape(n_f, L, C)
    x_raw = half(dot(normed, w_x)).reshape(n_f, L, C)
    bd = half(dot(normed, w_b))
    bc_raw = bd[:, :pair].reshape(n_f, L, pair)
    dt_raw = lanes_of(bd[:, pair:]).reshape(n_f, L, LANES)
    x_halo = half(dot(normed_edge, w_x)).reshape(n_f, EDGE, C)
    bc_halo = half(dot(normed_edge, w_b[:, :pair])).reshape(n_f, EDGE, pair)
    ggate = half(dot_t(cot_all, w_out)).reshape(n_f, L, C)

    def kernel_rows(kernel, bias):
        return jnp.concatenate([kernel, bias[None], jnp.zeros((8 - TAPS - 1, bias.shape[0]), F32)], 0)

    k_x = kernel_rows(mine(conv_weight[:, :DI], C, 1), mine(conv_bias[:DI], C, 0))
    k_b = kernel_rows(conv_weight[:, DI:], conv_bias[DI:])
    bias_lane = jnp.where(jnp.arange(LANES) < Hl, lanes_of(dt_bias), -100.0)
    heads = jnp.stack([bias_lane, jnp.exp(lanes_of(a_log)), lanes_of(d_skip)] + [jnp.zeros((LANES,), F32)] * 5)
    gain = jnp.broadcast_to(mine(norm_gain, C, 0)[None], (8, C))

    big, small = per(L, C), per(L, pair)
    lane, col_spec, row_spec, st = per(L, LANES), per(L, LANES), per(8, L), per(N, C)
    halo_x, halo_b = per(EDGE, C), per(EDGE, pair)
    kx_spec, kb_spec, h_spec, hr_spec = fixed(8, C), fixed(8, pair), fixed(8, LANES), per(HR, L)
    call = functools.partial(pl.pallas_call, grid=(n_f,), compiler_params=params(dimension_semantics=("arbitrary",)))

    state, through, pre_x, xd, pre_b, bc, cum, cum_row = call(
        enter_kernel,
        name="enter",
        in_specs=[big, halo_x, small, halo_b, lane, col_spec, kx_spec, kb_spec, h_spec],
        out_specs=[st, per(8, C), big, big, small, small, lane, hr_spec],
        out_shape=[
            shaped(n_f, N, C), shaped(n_f, 8, C), shaped(n_f, L, C), shaped(n_f, L, C, dtype=BF16),
            shaped(n_f, L, pair), shaped(n_f, L, pair, dtype=BF16), shaped(n_f, L, LANES), shaped(n_f, HR, L),
        ],
        scratch_shapes=[pltpu.VMEM((L + EDGE, C), F32), pltpu.VMEM((L + EDGE, pair), F32)],
    )(x_raw, x_halo, bc_raw, bc_halo, dt_raw, cols, k_x, k_b, heads)
    enter = chain(state, through, True, n_s)
    plain, mixed, sums = call(
        mix_kernel,
        name="mix",
        in_specs=[big, big, small, lane, hr_spec, col_spec, row_spec, st, big, big, kx_spec, h_spec],
        out_specs=[big, big, row_spec],
        out_shape=[shaped(n_f, L, C), shaped(n_f, L, C, dtype=BF16), shaped(n_f, 8, L)],
    )(pre_x, xd, bc, cum, cum_row, cols, seg_row, enter, z, ggate, gain, heads)
    total = total_over_fsdp(sums, n_f)
    ngate, dz, dy, d_enter, g_gain = call(
        functools.partial(gate_kernel, DI),
        name="gate",
        in_specs=[big, big, big, kx_spec, row_spec, lane, col_spec, small],
        out_specs=[big, big, big, st, kx_spec],
        out_shape=[shaped(n_f, L, C, dtype=BF16)] * 3 + [shaped(n_f, N, C), shaped(8, C)],
    )(mixed, z, ggate, gain, total, cum, cols, bc)
    grad = chain(d_enter, through, False, n_s)
    ngate, dz = ngate.reshape(T, C), dz.reshape(T, C)

    out_part = half(dot(ngate, w_out)).reshape(n_f, L, D)
    out_sum = lax.psum_scatter(out_part, "fsdp", scatter_dimension=0, tiled=True)[0]
    tok_float = tokens[0].astype(F32)
    output = half(tok_float + out_sum.astype(F32))
    g_out = lax.psum(half(t_dot(ngate, cot_all)), "seq").astype(F32)

    dx, db, dd, tail, halo, g_x, g_b, g_h = call(
        back_kernel,
        name="back",
        in_specs=[
            big, halo_x, small, halo_b, lane, col_spec, row_spec, kx_spec, kb_spec, h_spec,
            big, big, small, small, lane, hr_spec, st, st, big, big,
        ],
        out_specs=[big, small, lane, per(EDGE, C + pair), per(EDGE, C + pair), kx_spec, kb_spec, h_spec],
        out_shape=[
            shaped(n_f, L, C, dtype=BF16), shaped(n_f, L, pair, dtype=BF16), shaped(n_f, L, LANES, dtype=BF16),
            shaped(n_f, EDGE, C + pair), shaped(n_f, EDGE, C + pair, dtype=BF16), shaped(8, C), shaped(8, pair), shaped(8, LANES),
        ],
        scratch_shapes=[
            pltpu.VMEM((L + EDGE, C), F32), pltpu.VMEM((L + 2 * EDGE, C), F32),
            pltpu.VMEM((L + EDGE, pair), F32), pltpu.VMEM((L + 2 * EDGE, pair), F32),
            pltpu.VMEM((L, C), F32), pltpu.VMEM((L, L), F32),
        ],
    )(x_raw, x_halo, bc_raw, bc_halo, dt_raw, cols, seg_row, k_x, k_b, heads,
      pre_x, xd, pre_b, bc, cum, cum_row, enter, grad, plain, dy)
    got = lax.ppermute(halo, "seq", [(i + 1, i) for i in range(n_s - 1)])
    fixed_tail = half(tail + got.astype(F32))
    dx = lax.dynamic_update_slice(dx, fixed_tail[..., :C], (0, L - EDGE, 0)).reshape(T, C)
    db = lax.dynamic_update_slice(db, fixed_tail[..., C:], (0, L - EDGE, 0)).reshape(T, pair)
    dd48 = lax.dynamic_update_slice(jnp.zeros((T, H), BF16), dd.reshape(T, LANES)[:, :Hl], (0, f * Hl))
    dbd = jnp.concatenate([db, dd48], 1)

    gn_part = dot_t(dz, w_z) + dot_t(dx, w_x) + dot_t(dbd, w_b)
    gn = lax.psum_scatter(half(gn_part).reshape(n_f, L, D), "fsdp", scatter_dimension=0, tiled=True)[0].astype(F32)
    inv_rms = lax.rsqrt(jnp.mean(tok_float * tok_float, -1, keepdims=True) + EPSILON)
    scaled = tok_float * inv_rms
    grad_pre = jnp.sum(gn * scaled, 0)
    weighted = gn * pre_gain[None, :]
    input_grad = half(
        cotangent[0].astype(F32)
        + inv_rms * (weighted - scaled * jnp.mean(weighted * scaled, -1, keepdims=True))
    )

    packed = [half(t_dot(normed, v)).reshape(n_f, rows, v.shape[1]) for v in (dz, dx, dbd)]
    gz, gx, gb = [lax.all_to_all(v, "fsdp", 0, 0, tiled=True) for v in packed]
    g_in = jnp.concatenate(
        [
            gz.transpose(1, 0, 2).reshape(rows, DI),
            gx.transpose(1, 0, 2).reshape(rows, DI),
            half(jnp.sum(gb.astype(F32), 0)),
        ],
        1,
    )
    g_in = lax.psum(g_in, "seq").astype(F32)

    def place(values, full, width):
        zeros = jnp.zeros(values.shape[:-1] + (full,), F32)
        return lax.dynamic_update_slice_in_dim(zeros, values, f * width, zeros.ndim - 1)

    conv_w = jnp.concatenate([place(g_x[:TAPS], DI, C), g_b[:TAPS]], 1)
    conv_b = jnp.concatenate([place(g_x[TAPS], DI, C), g_b[TAPS]], 0)
    smalls = lax.psum(
        (
            grad_pre, conv_w, conv_b, place(g_h[0, :Hl], H, Hl), place(g_h[1, :Hl], H, Hl),
            place(g_h[2, :Hl], H, Hl), place(g_gain[0], DI, C),
        ),
        ("seq", "fsdp"),
    )
    return (output[None], input_grad[None], g_in, g_out) + tuple(smalls)


def solution(mesh):
    seq, row, rep = P("fsdp", "seq", None), P("fsdp", None), P()
    in_specs = (seq, row, rep, row, rep, rep, rep, rep, rep, rep, row, seq)
    out_specs = (seq, seq, row, row) + (rep,) * 7
    return jax.shard_map(shards, mesh=mesh, in_specs=in_specs, out_specs=out_specs, check_vma=False)
```

time: 1670 us -> 775 us (0.46)
  waiting for transfers between devices: 850 us -> 384 us
  local copies, waits for them, and re-layouts: 295 us -> 67.1 us
  other arithmetic: 236 us -> 32.2 us
  Pallas kernels: 0 us -> 193 us
  matrix products: 166 us -> 60.2 us
  blocking collectives: 72.3 us -> 0 us
    all_gather x7 -> x1, waiting for transfers between devices: 355 us -> 0.01 us  [shards(): cot_all = lax.all_gather(cot_own, 'fsdp').reshape(T, D)]
    pallas_call x0 -> x8, Pallas kernels: none -> 193 us  [the longest x1 75.1 us: gather(): pl.pallas_call(functools.partial(gather_kernel, n_s, n_f, C, DI), name='g...]
    psum x2, waiting for transfers between devices: 408 us -> 259 us  [the longest x1 130 us: shards(): lax.psum((grad_pre, conv_w, conv_b, place(g_h[0, :Hl], H, Hl), place(g_h[...]
    dot_general x17 -> x14, matrix products: 162 us -> 60.2 us  [the longest x4 22.7 us: t_dot(): lax.dot_general(a, b, (((0,), (0,)), ((), ())), preferred_element_type=F32)]
    unnamed x10 -> x7, waiting for transfers between devices: 2.7 us -> 81.4 us
    dynamic_slice x52 -> x7, local copies, waits for them, and re-layouts: 78 us -> 6.13 us  [mine(): return lax.dynamic_slice_in_dim(array, f * width, width, axis)]
    unnamed x8 -> x0, other arithmetic: 69.4 us -> none
    unnamed x270 -> x62, local copies, waits for them, and re-layouts: 67.6 us -> 19.1 us
  transfers between devices with their start and end apart: 15 -> 9, of which waited for: 8 -> 7; matrix products, arithmetic and copies ran while one was open for 21% -> 16% of each run, Pallas kernels for 0% -> 2%
where the time goes in v1:
time: 775 us; the launch traced here: 766 us
  waiting for transfers between devices  384 us (50%)
  Pallas kernels  193 us (25%)
  local copies, waits for them, and re-layouts  67.1 us (9%)
  matrix products  60.2 us (8%)
  other arithmetic  32.2 us (4%)
  between operations  14.7 us (2%)
  starting transfers between devices  14.5 us (2%)
    psum x1, waiting for transfers between devices, shards(): lax.psum((grad_pre, conv_w, conv_b, place(g_h[0, :Hl], H, Hl), place(g_h[...  130 us
    psum x1, waiting for transfers between devices, shards(): g_in = lax.psum(g_in, 'seq').astype(F32)  129 us
    unnamed x7, waiting for transfers between devices  81.4 us
    pallas_call x1, Pallas kernels, gather(): pl.pallas_call(functools.partial(gather_kernel, n_s, n_f, C, DI), name='g...  75.1 us
    pallas_call x2, Pallas kernels, chain(): pl.pallas_call(functools.partial(chain_kernel, n_s, forward), name='chain...  56.2 us
    all_to_all x3, waiting for transfers between devices, shards(): gz, gx, gb = [lax.all_to_all(v, 'fsdp', 0, 0, tiled=True) for v in packed]  43.7 us
    pallas_call x1, Pallas kernels, shards(): call(back_kernel, name='back', in_specs=[big, halo_x, small, halo_b, lane...  27.6 us
    dot_general x4, matrix products, t_dot(): lax.dot_general(a, b, (((0,), (0,)), ((), ())), preferred_element_type=F32)  22.7 us
  transfers between devices with their start and end apart: 9, of which 7 were waited for; matrix products, arithmetic and copies ran while one was open for 16% of the time, Pallas kernels for 2%

profile of v1, /device:TPU:0, one launch (start us, length us, event | category | flops | bytes accessed | tf_op | source)
XLA Modules:
  0.0 766.0 jit_solution(2852908305602921497)
XLA Ops:
  7.2 7.7 %copy.115.w = bf16[384,6448]{1,0:T(8,128)(2,1)} copy(bf16[384,6448]{0,1:T(8,128)(2,1)} %param.15) | data formatting | bytes 9904128 | tf_op args[3]
  14.9 75.1 %gather.1 = (bf16[4,256,1536]{2,1,0:T(8,128)(2,1)}, s32[4,1,2048]{2,1,0:T(1,128)}, bf16[4,384,768]{2,1,0:T(8,128)(2,1)}, bf16[4,384,768]{2,1,0:T(8,128)(2,1)}, b...) custom-call(bf16[256,1536]{1,0:T(8,128)(2,1)} %bitcast.111, s32[1,2048]{1,0:T(1,128)} %seg.1, ...), custom_call_target="tpu_custom_call" | custom-call | tf_op jit(solution)/shard_map/gather/pallas_call | solution.py:179
  121.1 4.8 stack.82.cols
  134.4 5.3 convolution_convert_fusion.4
  139.7 9.2 %enter.1 = (f32[4,128,768]{2,1,0:T(8,128)}, f32[4,8,768]{2,1,0:T(8,128)}, f32[4,256,768]{2,1,0:T(8,128)}, bf16[4,256,768]{2,1,0:T(8,128)(2,1)}, f32[4,256,256]{2...) custom-call(bf16[4,256,768]{2,1,0:T(8,128)(2,1)} %bitcast.114, ...), custom_call_target="tpu_custom_call" | custom-call | tf_op jit(solution)/shard_map/enter/pallas_call | solution.py:585
  148.9 7.3 chain_on.1.enter
  156.2 3.7 convolution_convert_fusion.3
  159.9 5.7 convolution_convert_fusion.2
  166.8 10.2 %mix.1 = (f32[4,256,768]{2,1,0:T(8,128)}, bf16[4,256,768]{2,1,0:T(8,128)(2,1)}, f32[4,8,256]{2,1,0:T(8,128)}) custom-call(f32[4,256,768]{2,1,0:T(8,128)} %get-tuple-element.47.pre_x, bf16[4,256,768]{2,1,0:T(8,128)(2,1)} %get-tuple-element.48.xd, bf16[4,256,256]{2,1,0:T(8,128)(2,1)} %get-tuple-element.49.bc, f32[4,256,128]{2,1,0:T(8,128)} %get-tuple-element.50.cum, ...), custom_call_target="tpu_custom_call" | custom-call | tf_op jit(solution)/shard_map/mix/pallas_call | solution.py:597
  176.9 6.4 total.1
  183.4 8.6 %gate.1 = (bf16[4,256,768]{2,1,0:T(8,128)(2,1)}, bf16[4,256,768]{2,1,0:T(8,128)(2,1)}, bf16[4,256,768]{2,1,0:T(8,128)(2,1)}, f32[4,128,768]{2,1,0:T(8,128)}, f32[8,768]{1,0:T(8,128)}) custom-call(bf16[4,256,768]{2,1,0:T(8,128)(2,1)} %get-tuple-element.56.mixed, bf16[4,256,768]{2,1,0:T(8,128)(2,1)} %bitcast.117, bf16[4,256,768]{2,1,0:T(8,128)(2,1)} %bitcast.119, ...), custom_call_target="tpu_custom_call" | custom-call | tf_op jit(solution)/shard_map/gate/pallas_call | solution.py:605
  192.0 48.9 %chain_back.1.grad = bf16[4,128,768]{2,1,0:T(8,128)(2,1)} custom-call(f32[4,128,768]{2,1,0:T(8,128)} %get-tuple-element.61.state, f32[4,8,768]{2,1,0:T(8,128)} %get-tuple-element.53.through), custom_call_target="tpu_custom_call" | custom-call | tf_op jit(solution)/shard_map/chain_back/pallas_call | solution.py:232
  240.9 27.6 %back.1 = (bf16[4,256,768]{2,1,0:T(8,128)(2,1)}, bf16[4,256,256]{2,1,0:T(8,128)(2,1)}, bf16[4,256,128]{2,1,0:T(8,128)(2,1)}, f32[4,8,1024]{2,1,0:T(8,128)}, bf16...) custom-call(bf16[4,256,768]{2,1,0:T(8,128)(2,1)} %bitcast.115, ...), custom_call_target="tpu_custom_call" | custom-call | tf_op jit(solution)/shard_map/back/pallas_call | solution.py:621
  281.8 6.5 bitcast_convert_fusion.2
  288.3 6.4 all-to-all-done.2
  294.7 4.5 all-to-all-start
  300.7 6.4 bitcast_convert_fusion.1
  307.1 21.0 %all-to-all-done = bf16[4,384,768]{2,1,0:T(8,128)(2,1)} async-done(((bf16[4,384,768]{2,1,0:T(8,128)(2,1)}), bf16[4,384,768]{2,1,0:T(8,128)(2,1)}, u32[]{:S(2)}, u32[]{:S(2)}) %all-to-all-start) | async-done | bytes 2359328 | tf_op jit(solution)/shard_map/all_to_all | solution.py:659
  328.1 4.5 all-to-all-start.1
  332.7 6.5 bitcast_convert_fusion
  340.1 4.3 copy.125
  344.4 16.3 %all-to-all-done.1 = bf16[4,384,768]{2,1,0:T(8,128)(2,1)} async-done(((bf16[4,384,768]{2,1,0:T(8,128)(2,1)}), bf16[4,384,768]{2,1,0:T(8,128)(2,1)}, u32[]{:S(2)}, u32[]{:S(2)}) %all-to-all-start.1) | async-done | bytes 2359328 | tf_op jit(solution)/shard_map/all_to_all | solution.py:659
  360.6 4.3 copy.127
  365.0 5.4 pad_maximum_fusion
  370.7 4.9 fusion.33
  378.3 3.6 add_convert_fusion
  382.0 5.5 convolution_convert_fusion
  394.0 129.4 %all-reduce.14.cloned.1.call-done = (bf16[384,6448]{0,1:T(8,128)(2,1)}, bf16[768,1536]{1,0:T(8,128)(2,1)}) async-done(((bf16[384,6448]{0,1:T(8,128)(2,1)}, bf16[768,1536]{1,0:T(8,128)(2,1)}), (bf16[384,6448]{0,1:T(8,128)(2,1)}, bf16[768,1536]{1,0:T(8,128)(2,1)})) %all-reduce.14.cloned.1.call-update) | async-done | bytes 7311376 | tf_op jit(solution)/shard_map/psum | solution.py:668
  523.4 7.1 convert_element_type.136
  533.4 36.9 %reduce-scatter.9.cloned.1.call-done = bf16[1,256,1536]{2,1,0:T(8,128)(2,1)} async-done(((bf16[4,256,1536]{2,1,0:T(8,128)(2,1)}), bf16[1,256,1536]{2,1,0:T(8,128)(2,1)}) %reduce-scatter.9.cloned.1.call-update) | async-done | bytes 786448
  572.7 44.4 %reduce-scatter.7.cloned.1.call-done = bf16[1,256,1536]{2,1,0:T(8,128)(2,1)} async-done(((bf16[4,256,1536]{2,1,0:T(8,128)(2,1)}), bf16[1,256,1536]{2,1,0:T(8,128)(2,1)}) %reduce-scatter.7.cloned.1.call-update) | async-done | bytes 786448
  620.5 129.7 %all-reduce.12.cloned.1.call-done = (f32[1536]{0:T(1024)}, f32[4,3328]{1,0:T(4,128)}, f32[3328]{0:T(1024)}, f32[48]{0:T(128)}, f32[48]{0:T(128)}, /*index=5*/f32[48]{0:T(128)}, f32[3072]{0:T(1024)}) async-done(((f32[1536]{0:T(1024)}, f32[4,3328]{1,0:T(4,128)}, f32[3328]{0:T(1024)}, f32[48]{0:T(128)}, f32[48]{0:T(128)}, /*index=5*/f32[48]{0:T(128)}, f32[3072]{0:T(1024)}), (f32[1536]{0:T(1024)}, ...) | async-done | bytes 85584 | tf_op jit(solution)/shard_map/psum | solution.py:676
  (159 shorter events, 83.1 us)
Async XLA Ops:
  7.2 152.7 %copy-start = (bf16[768,1536]{1,0:T(8,128)(2,1)S(1)}, bf16[768,1536]{1,0:T(8,128)(2,1)}, u32[]{:S(2)}) copy-start(bf16[768,1536]{1,0:T(8,128)(2,1)} %param.22) | copy-start | bytes 7077892
  7.2 152.7 %all-gather.3.cloned.1.call-start = ((), (), s32[]{:S(2)}) async-start(), calls=%async_computation.5 | async-start | bytes 3932160 | tf_op jit(solution)/shard_map/all_gather | solution.py:531
  90.0 2.8 copy-start.13
  90.1 2.8 copy-start.1
  93.7 1.7 copy-start.3
  94.2 2.1 copy-start.15
  94.2 2.7 copy-start.18
  94.2 3.3 copy-start.17
  121.1 5.7 copy-start.11
  121.1 7.8 %slice-start = ((f32[4,3328]{1,0:T(4,128)}), f32[4,256]{1,0:T(4,128)S(1)}, s32[]{:S(2)}) async-start(f32[4,3328]{1,0:T(4,128)} %param.16), calls=%async_computation.10 | async-start | bytes 8192 | tf_op jit(solution)/shard_map/slice | solution.py:574
  121.1 7.8 %slice-start.1 = ((f32[3328]{0:T(1024)}), f32[256]{0:T(256)S(1)}, s32[]{:S(2)}) async-start(f32[3328]{0:T(1024)} %param.17), calls=%async_computation.11 | async-start | bytes 2048 | tf_op jit(solution)/shard_map/slice | solution.py:574
  125.9 8.5 %copy-start.4 = (bf16[4,256,1536]{2,1,0:T(8,128)(2,1)S(1)}, bf16[4,256,1536]{2,1,0:T(8,128)(2,1)}, u32[]{:S(2)}) copy-start(bf16[4,256,1536]{2,1,0:T(8,128)(2,1)} %copy-done.3) | copy-start | bytes 9437188
  139.7 16.5 %copy-start.24 = (bf16[4,384,768]{2,1,0:T(8,128)(2,1)S(1)}, bf16[4,384,768]{2,1,0:T(8,128)(2,1)}, u32[]{:S(2)}) copy-start(bf16[4,384,768]{2,1,0:T(8,128)(2,1)} %get-tuple-element.54) | copy-start | bytes 7077892
  268.5 4.0 collective-permute-start
  278.3 16.4 %all-to-all-start.2 = ((bf16[4,384,304]{1,2,0:T(8,128)(2,1)}), bf16[4,384,304]{1,2,0:T(8,128)(2,1)S(1)}, u32[]{:S(2)}, u32[]{:S(2)}) async-start(bf16[4,384,304]{1,2,0:T(8,128)(2,1)} %bitcast.122), calls=%async_computation.2 | async-start | bytes 1867776 | tf_op jit(solution)/shard_map/all_to_all | solution.py:659
  294.7 33.4 %all-to-all-start = ((bf16[4,384,768]{2,1,0:T(8,128)(2,1)}), bf16[4,384,768]{2,1,0:T(8,128)(2,1)}, u32[]{:S(2)}, u32[]{:S(2)}) async-start(bf16[4,384,768]{2,1,0:T(8,128)(2,1)} %bitcast.135), calls=%async_computation | async-start | bytes 4718592 | tf_op jit(solution)/shard_map/all_to_all | solution.py:659
  328.1 32.5 %all-to-all-start.1 = ((bf16[4,384,768]{2,1,0:T(8,128)(2,1)}), bf16[4,384,768]{2,1,0:T(8,128)(2,1)}, u32[]{:S(2)}, u32[]{:S(2)}) async-start(bf16[4,384,768]{2,1,0:T(8,128)(2,1)} %bitcast.134), calls=%async_computation.1 | async-start | bytes 4718592 | tf_op jit(solution)/shard_map/all_to_all | solution.py:659
  332.6 190.8 %all-reduce.14.cloned.1.call-start = ((), (), s32[]{:S(2)}) async-start(), calls=%async_computation.9 | async-start | bytes 14622720 | tf_op jit(solution)/shard_map/psum | solution.py:668
  360.6 4.3 copy-start.9
  370.4 199.9 %reduce-scatter.9.cloned.1.call-start = ((), (), s32[]{:S(2)}) async-start(), calls=%async_computation.7 | async-start | bytes 3932160
  370.7 5.0 copy-start.6
  370.7 5.0 copy-start.25
  375.6 2.7 copy-start.8
  375.6 2.7 copy-start.10
  382.0 235.1 %reduce-scatter.7.cloned.1.call-start = ((), (), s32[]{:S(2)}) async-start(), calls=%async_computation.6 | async-start | bytes 3932160
  387.6 362.6 %all-reduce.12.cloned.1.call-start = ((), (), s32[]{:S(2)}) async-start(), calls=%async_computation.8 | async-start | bytes 183296 | tf_op jit(solution)/shard_map/psum | solution.py:676
  390.4 140.1 %copy-start.16 = (f32[3072]{0:T(1024)}, f32[3072]{0:T(1024)S(1)}, u32[]{:S(2)}) copy-start(f32[3072]{0:T(1024)S(1)} %dynamic_update_slice.35) | copy-start | bytes 36868
  391.8 138.7 %copy-start.22 = (f32[48]{0:T(128)}, f32[48]{0:T(128)S(1)}, u32[]{:S(2)}) copy-start(f32[48]{0:T(128)S(1)} %bitcast_dynamic-update-slice_fusion) | copy-start | bytes 580
  392.5 138.0 %copy-start.23 = (f32[48]{0:T(128)}, f32[48]{0:T(128)S(1)}, u32[]{:S(2)}) copy-start(f32[48]{0:T(128)S(1)} %bitcast_dynamic-update-slice_fusion.1) | copy-start | bytes 580
  393.3 137.2 %copy-start.21 = (f32[48]{0:T(128)}, f32[48]{0:T(128)S(1)}, u32[]{:S(2)}) copy-start(f32[48]{0:T(128)S(1)} %bitcast_dynamic-update-slice_fusion.2) | copy-start | bytes 580
  523.4 7.1 copy-start.5
  530.5 39.8 %copy-start.14 = (f32[1536]{0:T(1024)S(1)}, f32[1536]{0:T(1024)}, u32[]{:S(2)}) copy-start(f32[1536]{0:T(1024)} %param.14) | copy-start | bytes 18436
  (5 other events, 5.8 us)
Sparse Core Ops, SparseCore 0:
  90.2 43.3 all-gather.2
  370.5 152.8 all-reduce.13
  526.4 43.8 reduce-scatter.8
  573.1 43.8 reduce-scatter.6
  624.5 125.6 all-reduce.11
